TPU v7x, 32 devices: a whole 2x2x4 slice. The times are simulated.
32 devices in a mesh: vx: 4 (over y, x), vy: 8 (over z, core).
Axes of the slice: x: 2, y: 2, z: 4, core: 2. Of those that a mesh axis runs over, the one named last changes fastest.
Arguments:
- tokens: bfloat16 [96, 1, 256, 1024], P(('vx', 'vy')), may hold values from -256 to 256
- var_embed: bfloat16 [91, 1024], replicated, may hold values from -2 to 2
- query: bfloat16 [1024], replicated, may hold values from -6 to 6
- key_weight: bfloat16 [1024, 1024], P('vy'), may hold values from -1 to 1
- value_weight: bfloat16 [1024, 1024], P('vy'), may hold values from -0.1875 to 0.1875
- out_weight: bfloat16 [1024, 1024], P('vy'), may hold values from -0.1875 to 0.1875
- var_slot: int32 [91], replicated, may hold values from 0 to 95, as said below
Outputs:
- aggregated: bfloat16 [1, 256, 1024], P(None, ('vx', 'vy'))
Inputs may be any that keep to these rules, and one draw needn't show every extreme that they name: `var_slot`: distinct slot numbers; at least one device's slot holds a variable.
All inputs are finite; a program needn't handle non-finite values.
Results may differ from a plain program's by a relative error of at most 0.0096.
Values may be sent and summed in bfloat16 or wider, within the bound.
A program may use at most 64 MiB of HBM per device.

v0:
```python
import math

import jax
import jax.numpy as jnp
from jax import lax
from jax.sharding import PartitionSpec as P

HEADS = 16


def attend(keys, values, query_matrix, scale, heads):
    scores = (
        jnp.einsum("vbpd,dh->vbph", keys, query_matrix, preferred_element_type=jnp.float32) * scale
    )
    highest = jnp.max(scores, axis=0, keepdims=True)
    exponent = jnp.exp(scores - highest)
    weights = (exponent / jnp.sum(exponent, axis=0, keepdims=True)).astype(jnp.bfloat16)
    shaped = values.reshape(values.shape[:3] + (heads, values.shape[3] // heads))
    context = jnp.einsum("vbph,vbphe->bphe", weights, shaped, preferred_element_type=jnp.float32)
    return context.astype(jnp.bfloat16).reshape(values.shape[1:])


def shards(tokens, var_embed, query, key_weight, value_weight, out_weight, var_slot):
    slot_dev, batch, patches, width = tokens.shape
    heads = HEADS
    scale = 1.0 / math.sqrt(width // heads)
    count_y = lax.axis_size("vy")
    position = lax.axis_index("vx") * count_y + lax.axis_index("vy")
    local_slots = position * slot_dev + jnp.arange(slot_dev, dtype=jnp.int32)
    slot_match = (local_slots[:, None] == var_slot[None, :]).astype(jnp.bfloat16)
    embed_rows = jnp.dot(slot_match, var_embed, preferred_element_type=jnp.float32)
    mixed = (tokens.astype(jnp.float32) + embed_rows[:, None, None, :]).astype(jnp.bfloat16)
    key_full, value_full = (
        lax.all_gather(key_weight, "vy", axis=0, tiled=True),
        lax.all_gather(value_weight, "vy", axis=0, tiled=True),
    )
    stacked = jnp.stack((key_full, value_full))
    head_of = jnp.arange(width, dtype=jnp.int32) // (width // heads)
    query_matrix = jnp.where(
        head_of[:, None] == jnp.arange(heads, dtype=jnp.int32)[None, :],
        query[:, None],
        jnp.zeros((), jnp.bfloat16),
    )
    outgoing = mixed[None]
    selected = jnp.take(
        lax.all_to_all(outgoing, ("vx", "vy"), split_axis=3, concat_axis=1, tiled=True),
        var_slot,
        axis=1,
    )
    projected = jnp.einsum(
        "vbpd,cde->cvbpe", selected[0], stacked, preferred_element_type=jnp.float32
    ).astype(jnp.bfloat16)
    keys = projected[0]
    values = projected[1]
    context = attend(keys, values, query_matrix, scale, heads)
    flattened = context.reshape(-1, width)
    result = jnp.dot(
        flattened,
        lax.all_gather(out_weight, "vy", axis=0, tiled=True),
        preferred_element_type=jnp.float32,
    )
    return result.astype(jnp.bfloat16).reshape(batch, -1, width)


def solution(mesh):
    placed = (
        P(("vx", "vy"), None, None, None),
        P(),
        P(),
        P("vy", None),
        P("vy", None),
        P("vy", None),
        P(),
    )
    return jax.shard_map(
        shards, mesh=mesh, in_specs=placed, out_specs=P(None, ("vx", "vy"), None), check_vma=False
    )
```

profile of v0, /device:TPU:0, one launch (start us, length us, event | category | flops | bytes accessed | tf_op | source)
XLA Modules:
  0.0 141.9 jit_solution(14651676802304566514)
XLA Ops:
  6.5 0.0 copy-start
  6.5 0.0 all-gather.4.cloned.1.call-start
  6.5 0.7 all-gather.4.cloned.1.call-update
  7.3 0.0 all-gather.6.cloned.1.call-start
  7.3 0.7 all-gather.6.cloned.1.call-update
  8.0 0.0 copy-done
  8.0 0.9 fusion.27
  8.9 4.1 %fusion.5 = bf16[1,3,1,256,1024]{4,1,2,0,3:T(4,128)(2,1)} fusion(bf16[3,1,256,1024]{3,2,1,0:T(8,128)(2,1)} %param.7, f32[3,1024]{1,0:T(4,128)S(1)} %fusion.27), kind=kLoop, calls=%fused_computation.9 | loop fusion | flops 2359296 | bytes 3158016 | tf_op jit(solution)/shard_map/broadcast_in_dim | solution.py:44
  13.0 0.0 copy-start.4
  13.0 7.3 %all-to-all-start = ((bf16[1,3,1,256,1024]{4,1,2,0,3:T(4,128)(2,1)}), bf16[1,3,1,256,1024]{4,1,2,0,3:T(4,128)(2,1)S(1)}, u32[]{:S(2)}, u32[]{:S(2)}) async-start(bf16[1,3,1,256,1024]{4,1,2,0,3:T(4,128)(2,1)} %fusion.5), calls=%async_computation | async-start | bytes 4194304 | tf_op jit(solution)/shard_map/all_to_all | solution.py:46
  20.3 0.0 all-gather.8.cloned.1.call-start
  20.4 0.7 all-gather.8.cloned.1.call-update
  21.1 0.0 copy-done.4
  21.1 78.7 %all-to-all-done = bf16[1,3,1,256,1024]{4,1,2,0,3:T(4,128)(2,1)S(1)} async-done(((bf16[1,3,1,256,1024]{4,1,2,0,3:T(4,128)(2,1)}), bf16[1,3,1,256,1024]{4,1,2,0,3:T(4,128)(2,1)S(1)}, u32[]{:S(2)}, u32[]{:S(2)}) %all-to-all-start) | async-done | bytes 1572896 | tf_op jit(solution)/shard_map/all_to_all | solution.py:46
  99.8 0.6 copy.32
  100.4 0.1 copy.18
  100.5 0.7 gather_fusion
  101.3 0.2 broadcast_select_fusion
  101.5 0.0 all-gather.4.cloned.1.call-done
  101.5 1.6 %all-gather.6.cloned.1.call-done = bf16[1024,1024]{1,0:T(8,128)(2,1)} async-done(((bf16[128,1024]{1,0:T(8,128)(2,1)}), bf16[1024,1024]{1,0:T(8,128)(2,1)}) %all-gather.6.cloned.1.call-update) | async-done | bytes 2097168 | tf_op jit(solution)/shard_map/all_gather | solution.py:35
  103.1 6.0 %convert_bitcast_fusion = bf16[2,91,1,8,1024]{4,1,3,0,2:T(8,128)(2,1)S(1)} fusion(bf16[1,1024,1024]{2,1,0:T(8,128)(2,1)} %bitcast.56, bf16[1,1024,1024]{2,1,0:T(8,128)(2,1)} %bitcast.55, bf16[91,8,1024]{2,1,0:T(8,128)(2,1)S(1)} %broadcast_select_fusion), kind=kOutput, calls=%fused_computation.8 | convolution fusion | flops 3063332864 | bytes 8667136 | tf_op jit(solution)/shard_map/vbpd,cde->cvbpe/dot_general | solution.py:50
  109.1 0.0 copy-start.2
  109.1 1.7 %copy-done.2 = bf16[2,91,1,8,1024]{4,1,3,0,2:T(8,128)(2,1)} copy-done((bf16[2,91,1,8,1024]{4,1,3,0,2:T(8,128)(2,1)}, bf16[2,91,1,8,1024]{4,1,3,0,2:T(8,128)(2,1)S(1)}, u32[]{:S(2)}) %copy-start.2) | copy-done | bytes 2981912
  110.8 0.1 slice.11
  110.9 0.0 copy-start.3
  110.9 2.5 %copy.20 = bf16[1,91,1,8,1024]{1,4,3,2,0:T(8,128)(2,1)} copy(bf16[1,91,1,8,1024]{4,1,3,0,2:T(8,128)(2,1)S(1)} %slice.11) | data formatting | bytes 2981888 | tf_op jit(solution)/shard_map/slice | solution.py:54
  113.4 0.0 copy-done.3
  113.5 0.0 copy-start.1
  113.5 2.3 %fusion.14 = bf16[91,8,16,1]{0,2,1,3:T(8,128)(2,1)S(1)} fusion(bf16[2,91,1,8,1024]{4,1,3,0,2:T(8,128)(2,1)} %copy-done.2, s32[1024]{0:T(1024)S(1)} %add_select_fusion, bf16[1024]{0:T(1024)(128)(2,1)S(1)} %copy-done.3), kind=kOutput, calls=%fused_computation.21 | convolution fusion | flops 23934900 | bytes 1602304 | tf_op jit(solution)/shard_map/div | solution.py:17
  115.8 0.0 copy-done.1
  115.8 1.2 fusion.16
  117.0 0.1 reshape_reshape.3
  117.1 15.7 %all-gather.8.cloned.1.call-done = bf16[1024,1024]{1,0:T(8,128)(2,1)} async-done(((bf16[128,1024]{1,0:T(8,128)(2,1)}), bf16[1024,1024]{1,0:T(8,128)(2,1)}) %all-gather.8.cloned.1.call-update) | async-done | bytes 2097168 | tf_op jit(solution)/shard_map/all_gather | solution.py:59
  132.7 2.6 %fusion.15 = bf16[1,8,1024]{2,1,0:T(8,128)(2,1)} fusion(bf16[8,1024]{1,0:T(8,128)(2,1)S(1)} %reshape_reshape.3, bf16[1024,1024]{1,0:T(8,128)(2,1)} %all-gather.8.cloned.1.call-done), kind=kOutput, calls=%fused_computation.23 | convolution fusion | flops 16785408 | bytes 2129920 | tf_op jit(solution)/shard_map/dot_general | solution.py:57
  (6 shorter events, 0.0 us)
Async XLA Ops:
  6.5 1.5 %copy-start = (bf16[91,1024]{1,0:T(8,128)(2,1)S(1)}, bf16[91,1024]{1,0:T(8,128)(2,1)}, u32[]{:S(2)}) copy-start(bf16[91,1024]{1,0:T(8,128)(2,1)} %param.8) | copy-start | bytes 559108
  6.5 95.0 %all-gather.4.cloned.1.call-start = ((), (), s32[]{:S(2)}) async-start(), calls=%async_computation.1 | async-start | bytes 2359296 | tf_op jit(solution)/shard_map/all_gather | solution.py:34
  7.3 95.8 %all-gather.6.cloned.1.call-start = ((), (), s32[]{:S(2)}) async-start(), calls=%async_computation.2 | async-start | bytes 2359296 | tf_op jit(solution)/shard_map/all_gather | solution.py:35
  13.0 8.1 %copy-start.4 = (s32[91]{0:T(128)S(1)}, s32[91]{0:T(128)}, u32[]{:S(2)}) copy-start(s32[91]{0:T(128)} %param.13) | copy-start | bytes 1096
  13.0 86.8 %all-to-all-start = ((bf16[1,3,1,256,1024]{4,1,2,0,3:T(4,128)(2,1)}), bf16[1,3,1,256,1024]{4,1,2,0,3:T(4,128)(2,1)S(1)}, u32[]{:S(2)}, u32[]{:S(2)}) async-start(bf16[1,3,1,256,1024]{4,1,2,0,3:T(4,128)(2,1)} %fusion.5), calls=%async_computation | async-start | bytes 4194304 | tf_op jit(solution)/shard_map/all_to_all | solution.py:46
  20.3 112.4 %all-gather.8.cloned.1.call-start = ((), (), s32[]{:S(2)}) async-start(), calls=%async_computation.3 | async-start | bytes 2359296 | tf_op jit(solution)/shard_map/all_gather | solution.py:59
  109.1 1.7 %copy-start.2 = (bf16[2,91,1,8,1024]{4,1,3,0,2:T(8,128)(2,1)}, bf16[2,91,1,8,1024]{4,1,3,0,2:T(8,128)(2,1)S(1)}, u32[]{:S(2)}) copy-start(bf16[2,91,1,8,1024]{4,1,3,0,2:T(8,128)(2,1)S(1)} %convert_bitcast_fusion) | copy-start | bytes 8945668
  110.9 2.5 %copy-start.3 = (bf16[1024]{0:T(1024)(128)(2,1)S(1)}, bf16[1024]{0:T(1024)(128)(2,1)}, u32[]{:S(2)}) copy-start(bf16[1024]{0:T(1024)(128)(2,1)} %param.9) | copy-start | bytes 6148
  113.5 2.3 %copy-start.1 = (bf16[1,91,1,8,1024]{1,4,3,2,0:T(8,128)(2,1)S(1)}, bf16[1,91,1,8,1024]{1,4,3,2,0:T(8,128)(2,1)}, u32[]{:S(2)}) copy-start(bf16[1,91,1,8,1024]{1,4,3,2,0:T(8,128)(2,1)} %copy.20) | copy-start | bytes 4472836
Sparse Core Ops, SparseCore 0:
  8.9 49.8 all-gather.3
  60.4 42.6 all-gather.5
  104.7 28.0 all-gather.7
where the time goes:
time: 142 us
  waiting for transfers between devices  98 us (69%)
  between operations  13.3 us (9%)
  matrix products  13 us (9%)
  starting transfers between devices  7.41 us (5%)
  local copies, waits for them, and re-layouts  5.84 us (4%)
  other arithmetic  4.35 us (3%)
    all_to_all x1, waiting for transfers between devices, shards(): lax.all_to_all(outgoing, ('vx', 'vy'), split_axis=3, concat_axis=1, tiled...  78.7 us
    all_gather x1, waiting for transfers between devices, shards(): lax.all_gather(out_weight, 'vy', axis=0, tiled=True)  15.7 us
    all_to_all x1, starting transfers between devices, shards(): lax.all_to_all(outgoing, ('vx', 'vy'), split_axis=3, concat_axis=1, tiled...  7.33 us
    dot_general x1, matrix products, shards(): jnp.einsum('vbpd,cde->cvbpe', selected[0], stacked, preferred_element_typ...  6.04 us
    broadcast_in_dim x1, other arithmetic, shards(): outgoing = mixed[None]  4.11 us
  transfers between devices with their start and end apart: 4, of which 3 were waited for; matrix products, arithmetic and copies ran while one was open for 13% of the time, Pallas kernels for 0%

commit v1 on v0

v1 whole, which is shorter than its diff:
```python
import functools
import math

import jax
import jax.numpy as jnp
from jax import lax
from jax.experimental import pallas as pl
from jax.experimental.pallas import tpu as pltpu
from jax.sharding import PartitionSpec as P

HEADS = 16
CORES = 2
LOWEST = -1e38
F32 = jnp.float32
BF16 = jnp.bfloat16
MESH = pl.DeviceIdType.MESH
NT = (((1,), (1,)), ((), ()))


def split(x):
    high = x.astype(BF16)
    return high, (x - high.astype(F32)).astype(BF16)


def dot(a, b):
    return jnp.dot(a, b, preferred_element_type=F32)


def kernel(nx, ny, heads, tok, emb, qry, wk, wv, wo, slot, out,
           mixed, wbuf, kq_mine, kq_in, kq_all, ex, stat, st_in, st2, st2_in, fexp,
           part, in1, p2, in2, o3, in3,
           kq_s, kq_r, w_s, w_r, st_s, st_r, st2_s, st2_r, s1_s, s1_r, s2_s, s2_r, s3_s, s3_r):
    slots, patches, width = tok.shape
    rows = width // ny
    na = ny // CORES
    group = patches // nx
    piece = width // nx
    own = patches // (nx * ny)
    hdim = width // heads
    scale = 1.0 / math.sqrt(hdim)
    i = lax.axis_index("vx")
    j = lax.axis_index("vy")
    a = j // CORES
    c = j % CORES
    me = i * CORES + c
    vx_peers = [lax.rem(i + d, nx) for d in range(1, nx)]
    a_peers = [lax.rem(a + d, na) for d in range(1, na)]
    vy_peers = [lax.rem(j + d, ny) for d in range(1, ny)]
    nplane = nx * CORES
    plane = [lax.rem(me + d, nplane) for d in range(1, nplane)]

    def remote(src, dst, ss, rs, x, y):
        return pltpu.make_async_remote_copy(
            src_ref=src, dst_ref=dst, send_sem=ss, recv_sem=rs,
            device_id=(x, y), device_id_type=MESH)

    sent = []

    def send(*args):
        copy = remote(*args)
        copy.start()
        sent.append(copy)

    def arrived(ref, ss, rs):
        remote(ref, ref, ss, rs, i, j).wait_recv()

    barrier = pltpu.get_barrier_semaphore()
    for y in vy_peers:
        pl.semaphore_signal(barrier, inc=1, device_id=(i, y), device_id_type=MESH)
    for x in vx_peers:
        for d in range(CORES):
            pl.semaphore_signal(barrier, inc=1, device_id=(x, a * CORES + d), device_id_type=MESH)

    head_row = lax.broadcasted_iota(jnp.int32, (heads, width), 0)
    head_col = lax.broadcasted_iota(jnp.int32, (heads, width), 1) // hdim
    qmat = jnp.where(head_row == head_col, jnp.broadcast_to(qry[...].astype(F32), (heads, width)), 0.0).astype(BF16)
    kq = lax.dot_general(qmat, wk[...], NT, preferred_element_type=F32)
    kq_high, kq_low = split(kq)
    kq_mine[0] = kq_high
    kq_mine[1] = kq_low

    pl.semaphore_wait(barrier, (ny - 1) + (nx - 1) * CORES)

    for y in vy_peers:
        send(kq_mine, kq_in.at[j], kq_s, kq_r.at[j], i, y)
    col_i = pl.ds(pl.multiple_of(i * piece, 128), piece)
    row_j = pl.ds(pl.multiple_of(j * rows, rows), rows)
    for x in a_peers:
        send(wv.at[:, col_i], wbuf.at[row_j, col_i], w_s, w_r.at[0, a, i], i, x * CORES + c)
    partner = a * CORES + (1 - c)
    send(wv, wbuf.at[row_j, :], w_s, w_r.at[1, a, 0], i, partner)

    wbuf[row_j, :] = wv[...]
    kq_in[j] = kq_mine[...]

    count = slot.shape[1]
    ids = (i * ny + j) * slots + lax.broadcasted_iota(jnp.int32, (8, count), 0)
    match = jnp.where(ids == jnp.broadcast_to(slot[...], (8, count)), 1.0, 0.0)
    held = jnp.max(match, axis=1, keepdims=True)
    embed = dot(match.astype(BF16), emb[...])
    for s in range(slots):
        mixed[s * patches:(s + 1) * patches, :] = (tok[s].astype(F32) + embed[s:s + 1, :]).astype(BF16)

    for y in vy_peers:
        arrived(kq_in.at[y], kq_s, kq_r.at[y])
    for y in range(ny):
        kq_all[:, :, y * rows:(y + 1) * rows] = kq_in[y]
    scores = []
    top = jnp.full((patches, heads), LOWEST, F32)
    for s in range(slots):
        block = mixed[s * patches:(s + 1) * patches, :]
        score = scale * (lax.dot_general(block, kq_all[0], NT, preferred_element_type=F32)
                         + lax.dot_general(block, kq_all[1], NT, preferred_element_type=F32))
        score = jnp.where(held[s:s + 1, :] > 0, score, LOWEST)
        scores.append(score)
        top = jnp.maximum(top, score)
    total = jnp.zeros((patches, heads), F32)
    for s in range(slots):
        e = jnp.where(held[s:s + 1, :] > 0, jnp.exp(scores[s] - top), 0.0).astype(BF16)
        ex[s * patches:(s + 1) * patches, :] = e
        total += e.astype(F32)
    stat[:, 0:heads] = top
    stat[:, heads:2 * heads] = total

    def group_rows(x):
        return pl.ds(pl.multiple_of(x * group, group), group)

    for p in plane:
        x = p // CORES
        send(stat.at[group_rows(x), :], st_in.at[me], st_s, st_r.at[me], x, a * CORES + p % CORES)
    st_in[me] = stat[group_rows(i), :]

    for x in a_peers:
        rws = pl.ds(pl.multiple_of((x * CORES + c) * rows, rows), rows)
        here = wbuf.at[rws, col_i]
        arrived(here, w_s, w_r.at[0, x, i])
        for q in vx_peers:
            send(here, here, w_s, w_r.at[0, x, i], q, j)
        send(here, here, w_s, w_r.at[1, x, i], i, partner)

    for p in plane:
        arrived(st_in.at[p], st_s, st_r.at[p])
    tops = [st_in[p][:, 0:heads] for p in range(nplane)]
    high = functools.reduce(jnp.maximum, tops)
    st2[:, 0:heads] = high
    st2[:, heads:2 * heads] = sum(
        jnp.exp(tops[p] - high) * st_in[p][:, heads:2 * heads] for p in range(nplane))
    for x in a_peers:
        send(st2, st2_in.at[a], st2_s, st2_r.at[a], i, x * CORES + c)
    st2_in[a] = st2[...]

    for x in a_peers:
        rws = pl.ds(pl.multiple_of((x * CORES + c) * rows, rows), rows)
        for q in vx_peers:
            here = wbuf.at[rws, pl.ds(pl.multiple_of(q * piece, 128), piece)]
            arrived(here, w_s, w_r.at[0, x, q])
            send(here, here, w_s, w_r.at[1, x, q], i, partner)

    for x in a_peers:
        arrived(st2_in.at[x], st2_s, st2_r.at[x])
    highest = functools.reduce(jnp.maximum, [st2_in[p][:, 0:heads] for p in range(na)])
    whole = sum(jnp.exp(st2_in[p][:, 0:heads] - highest) * st2_in[p][:, heads:2 * heads] for p in range(na))
    k = lax.broadcasted_iota(jnp.int32, (heads, na * rows), 1)
    feature = ((k // rows) * CORES + c) * rows + k % rows
    spread = jnp.where(feature // hdim == lax.broadcasted_iota(jnp.int32, (heads, na * rows), 0), 1.0, 0.0).astype(BF16)
    for p in range(nplane):
        factor = jnp.exp(st_in[p][:, 0:heads] - highest) / whole
        f_high, f_low = split(factor)
        grown = dot(f_high, spread) + dot(f_low, spread)
        for x in range(na):
            fexp[x, p] = grown[:, x * rows:(x + 1) * rows]

    arrived(wbuf.at[pl.ds(pl.multiple_of(partner * rows, rows), rows), :], w_s, w_r.at[1, a, 0])
    for x in a_peers:
        rws = pl.ds(pl.multiple_of((x * CORES + 1 - c) * rows, rows), rows)
        for q in range(nx):
            arrived(wbuf.at[rws, q * piece:(q + 1) * piece], w_s, w_r.at[1, x, q])

    order = a_peers + [a]

    def project(x):
        wide = CORES * rows
        start = pl.multiple_of(x * wide, wide)
        col = start + lax.broadcasted_iota(jnp.int32, (heads, wide), 1)
        to_cols = jnp.where(col // hdim == lax.broadcasted_iota(jnp.int32, (heads, wide), 0), 1.0, 0.0).astype(BF16)
        value = dot(mixed[...], wbuf[:, pl.ds(start, wide)])
        value = value * dot(ex[...], to_cols)
        context = sum(value[s * patches:(s + 1) * patches] for s in range(slots)).astype(BF16)
        for g in range(nx):
            for d in range(CORES):
                part[x, g * CORES + d] = context[g * group:(g + 1) * group, d * rows:(d + 1) * rows]
        for p in plane:
            send(part.at[x, p], in1.at[x, me], s1_s, s1_r.at[x, me], p // CORES, a * CORES + p % CORES)

    def combine(x, last):
        for p in plane:
            arrived(in1.at[x, p], s1_s, s1_r.at[x, p])
        acc = fexp[x, me] * part[x, me].astype(F32)
        for p in plane:
            acc += fexp[x, p] * in1[x, p].astype(F32)
        if last:
            return acc
        p2[x] = acc.astype(BF16)
        send(p2.at[x], in2.at[a], s2_s, s2_r.at[a], i, x * CORES + c)

    project(order[0])
    for n in range(1, na):
        project(order[n])
        combine(order[n - 1], False)
    acc = combine(a, True)
    for x in a_peers:
        arrived(in2.at[x], s2_s, s2_r.at[x])
        acc += in2[x].astype(F32)
    result = dot(acc.astype(BF16), wo[...]).astype(BF16)
    for y in range(ny):
        o3[y] = result[y * own:(y + 1) * own]
    for y in vy_peers:
        send(o3.at[y], in3.at[j], s3_s, s3_r.at[j], i, y)
    final = o3[j].astype(F32)
    for y in vy_peers:
        arrived(in3.at[y], s3_s, s3_r.at[y])
        final += in3[y].astype(F32)
    out[...] = final.astype(BF16)
    for copy in sent:
        copy.wait_send()


def shards(tokens, var_embed, query, key_weight, value_weight, out_weight, var_slot):
    slots, batch, patches, width = tokens.shape
    nx, ny = lax.axis_size("vx"), lax.axis_size("vy")
    heads = HEADS
    rows, na, group, own = width // ny, ny // CORES, patches // nx, patches // (nx * ny)
    nplane = nx * CORES
    dma = pltpu.SemaphoreType.DMA
    vmem = pltpu.VMEM
    result = pl.pallas_call(
        functools.partial(kernel, nx, ny, heads),
        out_shape=jax.ShapeDtypeStruct((own, width), BF16),
        in_specs=[pl.BlockSpec(memory_space=pltpu.VMEM)] * 7,
        out_specs=pl.BlockSpec(memory_space=pltpu.VMEM),
        scratch_shapes=[
            vmem((slots * patches, width), BF16),
            vmem((width, width), BF16),
            vmem((2, heads, rows), BF16),
            vmem((ny, 2, heads, rows), BF16),
            vmem((2, heads, width), BF16),
            vmem((slots * patches, heads), BF16),
            vmem((patches, 2 * heads), F32),
            vmem((nplane, group, 2 * heads), F32),
            vmem((group, 2 * heads), F32),
            vmem((na, group, 2 * heads), F32),
            vmem((na, nplane, group, rows), F32),
            vmem((na, nplane, group, rows), BF16),
            vmem((na, nplane, group, rows), BF16),
            vmem((na, group, rows), BF16),
            vmem((na, group, rows), BF16),
            vmem((ny, own, width), BF16),
            vmem((ny, own, width), BF16),
            dma, dma((ny,)),
            dma, dma((2, na, nx)),
            dma, dma((nplane,)),
            dma, dma((na,)),
            dma, dma((na, nplane)),
            dma, dma((na,)),
            dma, dma((ny,)),
        ],
        compiler_params=pltpu.CompilerParams(
            collective_id=0, has_side_effects=True, vmem_limit_bytes=60 * 1024 * 1024),
    )(
        tokens.reshape(slots, batch * patches, width), var_embed, query.reshape(1, width),
        key_weight, value_weight, out_weight, var_slot.reshape(1, -1),
    )
    return result.reshape(batch, -1, width)


def solution(mesh):
    placed = (
        P(("vx", "vy"), None, None, None),
        P(),
        P(),
        P("vy", None),
        P("vy", None),
        P("vy", None),
        P(),
    )
    return jax.shard_map(
        shards, mesh=mesh, in_specs=placed, out_specs=P(None, ("vx", "vy"), None), check_vma=False
    )
```

time: 142 us -> 48.1 us (0.34)
  waiting for transfers between devices: 98 us -> 0 us
  Pallas kernels: 0 us -> 45.2 us
  between operations: 13.3 us -> 0.01 us
  matrix products: 13 us -> 0 us
  starting transfers between devices: 7.41 us -> 0 us
  other arithmetic: 4.35 us -> 0 us
  local copies, waits for them, and re-layouts: 5.84 us -> 2.6 us
    all_to_all x1 -> x0, waiting for transfers between devices: 78.7 us -> none  [shards(): lax.all_to_all(outgoing, ('vx', 'vy'), split_axis=3, concat_axis=1, tiled...]
    pallas_call x0 -> x1, Pallas kernels: none -> 45.2 us  [shards(): pl.pallas_call(functools.partial(kernel, nx, ny, heads), out_shape=jax.Sh...]
    all_gather x3 -> x0, waiting for transfers between devices: 17.3 us -> none  [the longest x1 15.7 us: shards(): lax.all_gather(out_weight, 'vy', axis=0, tiled=True)]
    dot_general x4 -> x0, matrix products: 10.6 us -> none  [the longest x1 6.04 us: shards(): jnp.einsum('vbpd,cde->cvbpe', selected[0], stacked, preferred_element_typ...]
    all_to_all x1 -> x0, starting transfers between devices: 7.33 us -> none  [shards(): lax.all_to_all(outgoing, ('vx', 'vy'), split_axis=3, concat_axis=1, tiled...]
    broadcast_in_dim x1 -> x0, other arithmetic: 4.11 us -> none  [shards(): outgoing = mixed[None]]
    slice x2 -> x0, local copies, waits for them, and re-layouts: 2.62 us -> none  [shards(): values = projected[1]]
    div x1 -> x0, matrix products: 2.32 us -> none  [attend(): exponent / jnp.sum(exponent, axis=0, keepdims=True)]
  transfers between devices with their start and end apart: 4 -> 0, of which waited for: 3 -> 0; matrix products, arithmetic and copies ran while one was open for 13% -> 0% of each run, Pallas kernels for 0% -> 0%
where the time goes in v1:
time: 48.1 us; the launch traced here: 47.8 us
  Pallas kernels  45.2 us (94%)
  local copies, waits for them, and re-layouts  2.6 us (5%)
    pallas_call x1, Pallas kernels, shards(): pl.pallas_call(functools.partial(kernel, nx, ny, heads), out_shape=jax.Sh...  45.2 us
    unnamed x1, local copies, waits for them, and re-layouts  1.32 us
    reshape x1, local copies, waits for them, and re-layouts, shards(): query.reshape(1, width)  1.28 us

profile of v1, /device:TPU:0, one launch (start us, length us, event | category | flops | bytes accessed | tf_op | source)
XLA Modules:
  0.0 47.8 jit_solution(2482297015170384610)
XLA Ops:
  0.0 1.3 %reshape.13.qry = bf16[1,1024]{1,0:T(2,128)(2,1)} reshape(bf16[1024]{0:T(1024)(128)(2,1)} %param.9) | data formatting | bytes 4096 | tf_op jit(solution)/shard_map/reshape | solution.py:270
  1.3 45.2 %shard_map.73 = bf16[8,1024]{1,0:T(8,128)(2,1)} custom-call(bf16[3,256,1024]{2,1,0:T(8,128)(2,1)} %bitcast.3, bf16[91,1024]{1,0:T(8,128)(2,1)} %emb.1, bf16[1,1024]{1,0:T(2,128)(2,1)} %reshape.13.qry, bf16[128,1024]{1,0:T(8,128)(2,1)} %wk.1, bf16[128,1024]{1,0:T(8,128)(2,1)} %wv.1, bf16[128,1024]{1,0:T(8,128)(2,1)} %wo.1, s32[1,91]{1,0:T(1,128)} %bitcast.5), custom_call_target="tpu_custom_call" | custom-call | tf_op jit(solution)/shard_map/pallas_call | solution.py:236
  46.5 1.3 %copy.9 = bf16[1,8,1024]{2,1,0:T(8,128)(2,1)} copy(bf16[1,8,1024]{2,1,0:T(8,128)(2,1)} %bitcast.4) | data formatting | bytes 32768

commit v2 on v1

--- a/solution.py
+++ b/solution.py
@@ -26,15 +26,17 @@
     return jnp.dot(a, b, preferred_element_type=F32)
 
 
-def kernel(nx, ny, heads, tok, emb, qry, wk, wv, wo, slot, out,
+def kernel(nx, ny, heads, tok_any, emb_any, qry_any, wk_any, wv_any, wo_any, slot_any, out,
+           tok, emb, qry, wk, wo, slot, load_s,
            mixed, wbuf, kq_mine, kq_in, kq_all, ex, stat, st_in, st2, st2_in, fexp,
            part, in1, p2, in2, o3, in3,
-           kq_s, kq_r, w_s, w_r, st_s, st_r, st2_s, st2_r, s1_s, s1_r, s2_s, s2_r, s3_s, s3_r):
+           kq_s, kq_r, w_s, w_r, wp_s, wp_r, st_s, st_r, st2_s, st2_r, s1_s, s1_r, s2_s, s2_r, s3_s, s3_r):
     slots, patches, width = tok.shape
     rows = width // ny
     na = ny // CORES
     group = patches // nx
-    piece = width // nx
+    piece = rows // nx
+    wide = CORES * rows
     own = patches // (nx * ny)
     hdim = width // heads
     scale = 1.0 / math.sqrt(hdim)
@@ -64,6 +66,13 @@
     def arrived(ref, ss, rs):
         remote(ref, ref, ss, rs, i, j).wait_recv()
 
+    row_j = pl.ds(pl.multiple_of(j * rows, rows), rows)
+    pairs = ((wk_any, wk), (qry_any, qry), (wv_any, wbuf.at[row_j, :]), (tok_any, tok),
+             (emb_any, emb), (slot_any, slot), (wo_any, wo))
+    loads = [pltpu.make_async_copy(src, dst, load_s.at[n]) for n, (src, dst) in enumerate(pairs)]
+    for load in loads:
+        load.start()
+
     barrier = pltpu.get_barrier_semaphore()
     for y in vy_peers:
         pl.semaphore_signal(barrier, inc=1, device_id=(i, y), device_id_type=MESH)
@@ -71,9 +80,11 @@
         for d in range(CORES):
             pl.semaphore_signal(barrier, inc=1, device_id=(x, a * CORES + d), device_id_type=MESH)
 
+    loads[0].wait()
+    loads[1].wait()
     head_row = lax.broadcasted_iota(jnp.int32, (heads, width), 0)
     head_col = lax.broadcasted_iota(jnp.int32, (heads, width), 1) // hdim
-    qmat = jnp.where(head_row == head_col, jnp.broadcast_to(qry[...].astype(F32), (heads, width)), 0.0).astype(BF16)
+    qmat = jnp.where(head_row == head_col, jnp.broadcast_to(qry[...].astype(F32).reshape(1, width), (heads, width)), 0.0).astype(BF16)
     kq = lax.dot_general(qmat, wk[...], NT, preferred_element_type=F32)
     kq_high, kq_low = split(kq)
     kq_mine[0] = kq_high
@@ -83,16 +94,26 @@
 
     for y in vy_peers:
         send(kq_mine, kq_in.at[j], kq_s, kq_r.at[j], i, y)
-    col_i = pl.ds(pl.multiple_of(i * piece, 128), piece)
-    row_j = pl.ds(pl.multiple_of(j * rows, rows), rows)
-    for x in a_peers:
-        send(wv.at[:, col_i], wbuf.at[row_j, col_i], w_s, w_r.at[0, a, i], i, x * CORES + c)
+
+    def block(x, d, q, n):
+        first = pl.multiple_of((x * CORES + d) * rows + q * piece, piece)
+        return wbuf.at[pl.ds(first, piece), pl.ds(pl.multiple_of(n * wide, wide), wide)]
+
+    def turn(x, step):
+        return lax.rem(x + 1 + step, na)
+
     partner = a * CORES + (1 - c)
-    send(wv, wbuf.at[row_j, :], w_s, w_r.at[1, a, 0], i, partner)
-
-    wbuf[row_j, :] = wv[...]
+    loads[2].wait()
+    for step in range(na):
+        for x in a_peers:
+            n = turn(x, step)
+            send(block(a, c, i, n), block(a, c, i, n), w_s, w_r.at[0, a, i, n], i, x * CORES + c)
+    send(wbuf.at[row_j, :], wbuf.at[row_j, :], wp_s, wp_r, i, partner)
+
     kq_in[j] = kq_mine[...]
 
+    for load in loads[3:]:
+        load.wait()
     count = slot.shape[1]
     ids = (i * ny + j) * slots + lax.broadcasted_iota(jnp.int32, (8, count), 0)
     match = jnp.where(ids == jnp.broadcast_to(slot[...], (8, count)), 1.0, 0.0)
@@ -108,9 +129,9 @@
     scores = []
     top = jnp.full((patches, heads), LOWEST, F32)
     for s in range(slots):
-        block = mixed[s * patches:(s + 1) * patches, :]
-        score = scale * (lax.dot_general(block, kq_all[0], NT, preferred_element_type=F32)
-                         + lax.dot_general(block, kq_all[1], NT, preferred_element_type=F32))
+        rows_s = mixed[s * patches:(s + 1) * patches, :]
+        score = scale * (lax.dot_general(rows_s, kq_all[0], NT, preferred_element_type=F32)
+                         + lax.dot_general(rows_s, kq_all[1], NT, preferred_element_type=F32))
         score = jnp.where(held[s:s + 1, :] > 0, score, LOWEST)
         scores.append(score)
         top = jnp.maximum(top, score)
@@ -130,13 +151,33 @@
         send(stat.at[group_rows(x), :], st_in.at[me], st_s, st_r.at[me], x, a * CORES + p % CORES)
     st_in[me] = stat[group_rows(i), :]
 
-    for x in a_peers:
-        rws = pl.ds(pl.multiple_of((x * CORES + c) * rows, rows), rows)
-        here = wbuf.at[rws, col_i]
-        arrived(here, w_s, w_r.at[0, x, i])
-        for q in vx_peers:
-            send(here, here, w_s, w_r.at[0, x, i], q, j)
-        send(here, here, w_s, w_r.at[1, x, i], i, partner)
+    def share(step):
+        n = turn(a, step)
+        for x in a_peers:
+            here = block(x, c, i, n)
+            arrived(here, w_s, w_r.at[0, x, i, n])
+            for q in vx_peers:
+                send(here, here, w_s, w_r.at[0, x, i, n], q, j)
+            send(here, here, w_s, w_r.at[1, x, i, n], i, partner)
+
+    def hand_over(step):
+        n = turn(a, step)
+        for x in a_peers:
+            for q in vx_peers:
+                here = block(x, c, q, n)
+                arrived(here, w_s, w_r.at[0, x, q, n])
+                send(here, here, w_s, w_r.at[1, x, q, n], i, partner)
+
+    def complete(step):
+        n = turn(a, step)
+        for x in a_peers:
+            for q in range(nx):
+                arrived(block(x, 1 - c, q, n), w_s, w_r.at[1, x, q, n])
+
+    share(0)
+    if na > 1:
+        share(1)
+    hand_over(0)
 
     for p in plane:
         arrived(st_in.at[p], st_s, st_r.at[p])
@@ -149,12 +190,39 @@
         send(st2, st2_in.at[a], st2_s, st2_r.at[a], i, x * CORES + c)
     st2_in[a] = st2[...]
 
-    for x in a_peers:
-        rws = pl.ds(pl.multiple_of((x * CORES + c) * rows, rows), rows)
-        for q in vx_peers:
-            here = wbuf.at[rws, pl.ds(pl.multiple_of(q * piece, 128), piece)]
-            arrived(here, w_s, w_r.at[0, x, q])
-            send(here, here, w_s, w_r.at[1, x, q], i, partner)
+    order = a_peers + [a]
+
+    def project(x):
+        start = pl.multiple_of(x * wide, wide)
+        col = start + lax.broadcasted_iota(jnp.int32, (heads, wide), 1)
+        to_cols = jnp.where(col // hdim == lax.broadcasted_iota(jnp.int32, (heads, wide), 0), 1.0, 0.0).astype(BF16)
+        value = dot(mixed[...], wbuf[:, pl.ds(start, wide)])
+        value = value * dot(ex[...], to_cols)
+        context = sum(value[s * patches:(s + 1) * patches] for s in range(slots)).astype(BF16)
+        for g in range(nx):
+            for d in range(CORES):
+                part[x, g * CORES + d] = context[g * group:(g + 1) * group, d * rows:(d + 1) * rows]
+        for p in plane:
+            send(part.at[x, p], in1.at[x, me], s1_s, s1_r.at[x, me], p // CORES, a * CORES + p % CORES)
+
+    def combine(x, last):
+        for p in plane:
+            arrived(in1.at[x, p], s1_s, s1_r.at[x, p])
+        acc = fexp[x, me] * part[x, me].astype(F32)
+        for p in plane:
+            acc += fexp[x, p] * in1[x, p].astype(F32)
+        if last:
+            return acc
+        p2[x] = acc.astype(BF16)
+        send(p2.at[x], in2.at[a], s2_s, s2_r.at[a], i, x * CORES + c)
+
+    arrived(wbuf.at[pl.ds(pl.multiple_of(partner * rows, rows), rows), :], wp_s, wp_r)
+    complete(0)
+    project(order[0])
+    if na > 2:
+        share(2)
+    if na > 1:
+        hand_over(1)
 
     for x in a_peers:
         arrived(st2_in.at[x], st2_s, st2_r.at[x])
@@ -170,42 +238,13 @@
         for x in range(na):
             fexp[x, p] = grown[:, x * rows:(x + 1) * rows]
 
-    arrived(wbuf.at[pl.ds(pl.multiple_of(partner * rows, rows), rows), :], w_s, w_r.at[1, a, 0])
-    for x in a_peers:
-        rws = pl.ds(pl.multiple_of((x * CORES + 1 - c) * rows, rows), rows)
-        for q in range(nx):
-            arrived(wbuf.at[rws, q * piece:(q + 1) * piece], w_s, w_r.at[1, x, q])
-
-    order = a_peers + [a]
-
-    def project(x):
-        wide = CORES * rows
-        start = pl.multiple_of(x * wide, wide)
-        col = start + lax.broadcasted_iota(jnp.int32, (heads, wide), 1)
-        to_cols = jnp.where(col // hdim == lax.broadcasted_iota(jnp.int32, (heads, wide), 0), 1.0, 0.0).astype(BF16)
-        value = dot(mixed[...], wbuf[:, pl.ds(start, wide)])
-        value = value * dot(ex[...], to_cols)
-        context = sum(value[s * patches:(s + 1) * patches] for s in range(slots)).astype(BF16)
-        for g in range(nx):
-            for d in range(CORES):
-                part[x, g * CORES + d] = context[g * group:(g + 1) * group, d * rows:(d + 1) * rows]
-        for p in plane:
-            send(part.at[x, p], in1.at[x, me], s1_s, s1_r.at[x, me], p // CORES, a * CORES + p % CORES)
-
-    def combine(x, last):
-        for p in plane:
-            arrived(in1.at[x, p], s1_s, s1_r.at[x, p])
-        acc = fexp[x, me] * part[x, me].astype(F32)
-        for p in plane:
-            acc += fexp[x, p] * in1[x, p].astype(F32)
-        if last:
-            return acc
-        p2[x] = acc.astype(BF16)
-        send(p2.at[x], in2.at[a], s2_s, s2_r.at[a], i, x * CORES + c)
-
-    project(order[0])
     for n in range(1, na):
+        complete(n)
         project(order[n])
+        if n + 2 < na:
+            share(n + 2)
+        if n + 1 < na:
+            hand_over(n + 1)
         combine(order[n - 1], False)
     acc = combine(a, True)
     for x in a_peers:
@@ -236,9 +275,16 @@
     result = pl.pallas_call(
         functools.partial(kernel, nx, ny, heads),
         out_shape=jax.ShapeDtypeStruct((own, width), BF16),
-        in_specs=[pl.BlockSpec(memory_space=pltpu.VMEM)] * 7,
+        in_specs=[pl.BlockSpec(memory_space=pl.ANY)] * 7,
         out_specs=pl.BlockSpec(memory_space=pltpu.VMEM),
         scratch_shapes=[
+            vmem((slots, batch * patches, width), BF16),
+            vmem(var_embed.shape, BF16),
+            vmem((width,), BF16),
+            vmem((rows, width), BF16),
+            vmem((rows, width), BF16),
+            vmem((1, var_slot.shape[0]), jnp.int32),
+            dma((7,)),
             vmem((slots * patches, width), BF16),
             vmem((width, width), BF16),
             vmem((2, heads, rows), BF16),
@@ -257,7 +303,8 @@
             vmem((ny, own, width), BF16),
             vmem((ny, own, width), BF16),
             dma, dma((ny,)),
-            dma, dma((2, na, nx)),
+            dma, dma((2, na, nx, na)),
+            dma, dma,
             dma, dma((nplane,)),
             dma, dma((na,)),
             dma, dma((na, nplane)),
@@ -267,7 +314,7 @@
         compiler_params=pltpu.CompilerParams(
             collective_id=0, has_side_effects=True, vmem_limit_bytes=60 * 1024 * 1024),
     )(
-        tokens.reshape(slots, batch * patches, width), var_embed, query.reshape(1, width),
+        tokens.reshape(slots, batch * patches, width), var_embed, query,
         key_weight, value_weight, out_weight, var_slot.reshape(1, -1),
     )
     return result.reshape(batch, -1, width)

time: 48.1 us -> 44.3 us (0.921)
  Pallas kernels: 45.2 us -> 42.7 us
  local copies, waits for them, and re-layouts: 2.6 us -> 1.32 us
    pallas_call x1, Pallas kernels: 45.2 us -> 42.7 us  [shards(): pl.pallas_call(functools.partial(kernel, nx, ny, heads), out_shape=jax.Sh...]
    reshape x1 -> x0, local copies, waits for them, and re-layouts: 1.28 us -> none  [shards(): query.reshape(1, width)]
where the time goes in v2:
time: 44.3 us; the launch traced here: 44.1 us
  Pallas kernels  42.7 us (96%)
  local copies, waits for them, and re-layouts  1.32 us (3%)
    pallas_call x1, Pallas kernels, shards(): pl.pallas_call(functools.partial(kernel, nx, ny, heads), out_shape=jax.Sh...  42.7 us
    unnamed x1, local copies, waits for them, and re-layouts  1.32 us

profile of v2, /device:TPU:0, one launch (start us, length us, event | category | flops | bytes accessed | tf_op | source)
XLA Modules:
  0.0 44.1 jit_solution(2454148676028063617)
XLA Ops:
  0.0 42.7 %shard_map.73 = bf16[8,1024]{1,0:T(8,128)(2,1)} custom-call(bf16[3,256,1024]{2,1,0:T(8,128)(2,1)} %bitcast.3, bf16[91,1024]{1,0:T(8,128)(2,1)} %emb_any.1, bf16[1024]{0:T(1024)(128)(2,1)} %qry_any.1, bf16[128,1024]{1,0:T(8,128)(2,1)} %wk_any.1, bf16[128,1024]{1,0:T(8,128)(2,1)} %wv_any.1, bf16[128,1024]{1,0:T(8,128)(2,1)} %wo_any.1, s32[1,91]{1,0:T(1,128)} %bitcast.5), custom_call_target="tpu_custom_call" | custom-call | tf_op jit(solution)/shard_map/pallas_call | solution.py:275
  42.7 1.3 %copy.9 = bf16[1,8,1024]{2,1,0:T(8,128)(2,1)} copy(bf16[1,8,1024]{2,1,0:T(8,128)(2,1)} %bitcast.4) | data formatting | bytes 32768
